TPU v7x, 32 devices: a whole 2x2x4 slice. The times are simulated.
32 devices in a mesh: dp: 8 (over z, y), tensor: 4 (over x, core).
Axes of the slice: x: 2, y: 2, z: 4, core: 2. Of those that a mesh axis runs over, the one named last changes fastest.
Arguments:
- sampled_earlier_tokens: int32 [32, 169], P('dp'), may hold values from 0 to 4095
- quantizer_vectors: float32 [4096, 32], replicated, may hold values from -6 to 6
- summed_latent_canvas: float32 [32, 256, 32], P('dp'), may hold values from -6 to 6
- latent_lift_matrix: float32 [32, 1536], replicated, may hold values from -1 to 1
- location_tier_offset: float32 [256, 1536], replicated, may hold values from -3 to 3
- adaptive_norm_factors: float32 [1, 32, 6, 1536], P(None, 'dp'), may hold values from -3 to 3
- logit_sharpness: float32 [1, 16], P(None, 'tensor'), may hold values from 2 to 240, as said below
- probe_match_content_matrix: bfloat16 [1, 1536, 3, 1536], P(None, 'dp', None, 'tensor'), may hold values from -1 to 1, as said below
- mixing_projection_matrix: bfloat16 [1, 1536, 1536], P(None, 'tensor', 'dp'), may hold values from -0.15625 to 0.15625
- widening_projection_matrix: bfloat16 [1, 1536, 6144], P(None, 'dp', 'tensor'), may hold values from -0.15625 to 0.15625
- narrowing_projection_matrix: bfloat16 [1, 6144, 1536], P(None, 'tensor', 'dp'), may hold values from -0.078125 to 0.078125
- cached_lower_grid_lookups: bfloat16 [1, 32, 424, 1536], P(None, 'dp', None, 'tensor'), may hold values from -6 to 6
- cached_lower_grid_payloads: bfloat16 [1, 32, 424, 1536], P(None, 'dp', None, 'tensor'), may hold values from -6 to 6
- final_norm_factors: float32 [32, 2, 1536], P('dp'), may hold values from -3 to 3
- vocabulary_logit_matrix: bfloat16 [1536, 4096], P(None, 'tensor'), may hold values from -0.15625 to 0.15625
Outputs:
- logits: bfloat16 [32, 256, 4096], P('dp', None, 'tensor')
- canvas: float32 [32, 256, 32], P('dp')
Inputs may be any that keep to these rules, and one draw needn't show every extreme that they name: `logit_sharpness`: Positive. `probe_match_content_matrix`: entries of spread about 1536 ** -0.5.
All inputs are finite; a program needn't handle non-finite values.
Results may differ from a plain program's by a relative error of at most 0.015.
Values may be sent and summed in bfloat16 or wider, within the bound.
A program may use at most 128 MiB of HBM per device.

v0:
```python
import functools
from types import SimpleNamespace
from typing import Any, NamedTuple

import jax
import jax.numpy as jnp
import numpy as np
from jax import lax
from jax.experimental import pallas as pl
from jax.experimental.pallas import tpu as pltpu
from jax.sharding import PartitionSpec as P

SIDE = 16
PREV = 13
MESH = pl.DeviceIdType.MESH
norm_floor = 0.1
highest = lax.Precision.HIGHEST
bf16 = jnp.bfloat16
f32 = jnp.float32


def interp_matrix(grid_side, prev_side):
    out_cells = np.arange(grid_side)
    numerator = np.maximum((2 * out_cells + 1) * prev_side - grid_side, 0)
    lower_cell = numerator // (2 * grid_side)
    fraction = (numerator % (2 * grid_side)) / (2.0 * grid_side)
    upper_cell = np.minimum(lower_cell + 1, prev_side - 1)
    in_cells = np.arange(prev_side)
    lower_hit = (in_cells[None, :] == lower_cell[:, None]).astype(np.float64)
    upper_hit = (in_cells[None, :] == upper_cell[:, None]).astype(np.float64)
    return lower_hit * (1.0 - fraction)[:, None] + upper_hit * fraction[:, None]


def modulate(stream, scale_vec, shift_vec):
    center = stream - jnp.mean(stream, axis=-1, keepdims=True)
    variance = jnp.mean(center * center, axis=-1, keepdims=True)
    return center * lax.rsqrt(variance + norm_floor) * (1.0 + scale_vec) + shift_vec


def unit(vectors):
    return vectors * lax.rsqrt(jnp.sum(vectors * vectors, axis=-1, keepdims=True) + 1.0)


def dot(left, right):
    return jnp.dot(left, right, preferred_element_type=f32)


def dot_t(left, right):
    return lax.dot_general(left, right, (((1,), (1,)), ((), ())), preferred_element_type=f32)


def loop(total, body, scope=None):
    def step(index, carry):
        if scope is None:
            body(index)
        else:
            with jax.named_scope(scope):
                body(index)
        return carry

    lax.fori_loop(0, total, step, 0)


QKV, OUT, UP, DOWN = range(4)
EARLY = ((UP, 0), (DOWN, 0))


class Relay:
    def __init__(self, outer, shard_rows, buffers, parts, early, sems):
        self.outer, self.rows, self.buffers, self.parts = outer, shard_rows, buffers, parts
        self.early = early
        self.dp, self.t = lax.axis_index("dp"), lax.axis_index("tensor")
        self.o, self.p = self.dp // 2, lax.rem(self.dp, 2)
        self.z_recv, self.up_send, self.down_send, self.y_recv, self.y_send = sems
        self.number = {}
        for matrix, count in enumerate(parts):
            for part in range(count):
                self.number[(matrix, part)] = len(self.number)

    def ref(self, chunk, o, plane):
        matrix, part = chunk
        count = self.parts[matrix]
        rows = self.rows // count
        p = self.p if plane == 0 else 1 - self.p
        if matrix == DOWN:
            part = part + p * (count - 1 - 2 * part)
        if matrix == QKV:
            start = (o * 2 + p) * self.rows
            rows = self.rows
            return self.buffers[matrix].at[part, pl.ds(pl.multiple_of(start, rows), rows)]
        start = (o * 2 + p) * self.rows + part * rows
        return self.buffers[matrix].at[pl.ds(pl.multiple_of(start, rows), rows)]

    def copy(self, way, chunk, src, plane):
        ref = self.ref(chunk, src, plane)
        number = self.number[chunk]
        if way == "y":
            target = self.o * 2 + 1 - self.p
            send, recv = self.y_send.at[number, src], self.y_recv.at[number, src]
        else:
            target = self.dp + 2 if way == "up" else self.dp - 2
            sends = self.up_send if way == "up" else self.down_send
            send, recv = sends.at[number, plane, src], self.z_recv.at[number, plane, src]
        return pltpu.make_async_remote_copy(
            src_ref=ref, dst_ref=ref, send_sem=send, recv_sem=recv,
            device_id=(target, self.t), device_id_type=MESH,
        )

    def sends(self, way, chunk, src, plane, act):
        room = {"up": self.o < self.outer - 1, "down": self.o > 0, "y": None}[way]
        if room is None:
            act(self.copy(way, chunk, src, plane))
        else:
            pl.when(room)(lambda: act(self.copy(way, chunk, src, plane)))

    def crosses_early(self, chunk):
        return chunk in self.early

    def start_y(self, chunk, act=lambda copy: copy.start()):
        self.sends("y", chunk, self.o, 0, act)

    def start_z(self, chunk, plane=0, act=lambda copy: copy.start()):
        for way in ("up", "down"):
            self.sends(way, chunk, self.o, plane, act)

    def own_z(self, chunks):
        for chunk in chunks:
            self.start_z(chunk)

    def own_y(self, chunks):
        for chunk in chunks:
            if not self.crosses_early(chunk):
                self.start_y(chunk)

    def cross_z(self, chunks):
        for chunk in chunks:
            if self.crosses_early(chunk):
                self.wait_y(chunk, self.o)
                self.start_z(chunk, 1)

    def cross_rest(self, chunks):
        def rest(src):
            @pl.when(src != self.o)
            def _():
                for chunk in chunks:
                    self.sends("y", chunk, src, 0, lambda copy: copy.start())

        loop(self.outer, rest)

    def wait_y(self, chunk, src):
        ref = self.ref(chunk, src, 1)
        number = self.number[chunk]
        pltpu.make_async_remote_copy(
            src_ref=ref, dst_ref=ref, send_sem=self.y_send.at[number, src],
            recv_sem=self.y_recv.at[number, src],
            device_id=(self.o * 2 + 1 - self.p, self.t), device_id_type=MESH,
        ).wait_recv()

    def wait_y_all(self, chunks):
        with jax.named_scope("wait_y"):
            self.wait_y_each(chunks)

    def wait_y_each(self, chunks):
        for chunk in chunks:
            if not self.crosses_early(chunk):
                loop(self.outer, lambda src: self.wait_y(chunk, src))

    def step(self, chunks, s):
        with jax.named_scope("relay"):
            self.step_inner(chunks, s)

    def step_inner(self, chunks, s):
        for chunk in chunks:
            early = self.crosses_early(chunk)
            for plane in (0, 1) if early else (0,):
                for way, src, there in (
                    ("up", self.o - s, self.o >= s),
                    ("down", self.o + s, self.o + s < self.outer),
                ):

                    @pl.when(there)
                    def _():
                        ref = self.ref(chunk, src, plane)
                        number = self.number[chunk]
                        pltpu.make_async_remote_copy(
                            src_ref=ref, dst_ref=ref,
                            send_sem=self.up_send.at[number, plane, src],
                            recv_sem=self.z_recv.at[number, plane, src],
                            device_id=(self.o * 2 + 1 - self.p, self.t), device_id_type=MESH,
                        ).wait_recv()
                        self.sends(way, chunk, src, plane, lambda copy: copy.start())
                        if not early and chunk[0] != OUT:
                            self.sends("y", chunk, src, plane, lambda copy: copy.start())

    def steps(self, chunks, third):
        span = self.outer - 1
        low, high = 1 + third * span // 3, 1 + (third + 1) * span // 3
        if high - low == 1:
            self.step(chunks, low)
        elif high > low:
            loop(high - low, lambda index: self.step(chunks, low + index))

    def drain(self):
        def done(copy):
            copy.wait_send()

        for chunk in self.number:
            early = self.crosses_early(chunk)
            for plane in (0, 1) if early else (0,):

                def sent(src):
                    @pl.when(src <= self.o)
                    def _():
                        self.sends("up", chunk, src, plane, done)

                    @pl.when(src >= self.o)
                    def _():
                        self.sends("down", chunk, src, plane, done)

                    if not early:
                        self.sends("y", chunk, src, plane, done)

                loop(self.outer, sent)
            if early:
                self.start_y(chunk, done)


class Given(NamedTuple):
    ids: Any
    codes: Any
    summed: Any
    lift: Any
    offset: Any
    factors: Any
    sharp: Any
    qkv: Any
    out: Any
    up: Any
    down: Any
    keys: Any
    values: Any
    head_factors: Any
    vocab: Any
    grow: Any


INPUTS = Given._fields


def scratch_shapes(dims):
    outer, rows, images, tokens = dims.outer, dims.rows, dims.images, dims.tokens
    width, heads_width, units = dims.width, dims.heads_width, dims.units
    prev, channels, vocab, codes = dims.prev, dims.channels, dims.vocab, dims.codes
    cache, half, blocks = dims.cache, dims.half, dims.blocks
    chunks = sum(dims.parts)
    dma = pltpu.SemaphoreType.DMA
    block = width // blocks
    return dict(
        w_qkv=pltpu.VMEM((3, width, heads_width), bf16),
        w_out=pltpu.VMEM((width, heads_width), bf16),
        w_up=pltpu.VMEM((width, units), bf16),
        w_down=pltpu.VMEM((width, units), bf16),
        s_ids=pltpu.VMEM((images, prev), jnp.int32),
        s_codes=pltpu.VMEM((channels, codes), f32),
        code_parts=pltpu.VMEM((3 * channels, codes), bf16),
        s_summed=pltpu.VMEM((images, channels, tokens), f32),
        canvas_v=pltpu.VMEM((images, channels, tokens), f32),
        s_lift=pltpu.VMEM((channels, width), f32),
        s_offset=pltpu.VMEM((tokens, width), f32),
        s_factors=pltpu.VMEM((6, images, width), f32),
        s_head_factors=pltpu.VMEM((images, 2, width), f32),
        s_keys=pltpu.VMEM((images, cache, heads_width), bf16),
        s_values=pltpu.VMEM((images, cache, heads_width), bf16),
        all_keys=pltpu.VMEM((images, dims.heads, tokens + cache, heads_width // dims.heads), bf16),
        all_values=pltpu.VMEM((images, dims.heads, tokens + cache, 128), bf16),
        s_vocab=pltpu.VMEM((width, vocab), bf16),
        s_grow=pltpu.VMEM((tokens, prev), f32),
        normed=pltpu.VMEM((images, tokens, width), bf16),
        normed2=pltpu.VMEM((images, tokens, width), bf16),
        normed3=pltpu.VMEM((images, tokens, width), bf16),
        gain=pltpu.VMEM((half, 1, width), f32),
        stream=pltpu.VMEM((half, tokens, width), f32),
        projected=pltpu.VMEM((tokens, 3 * heads_width), f32),
        attended=pltpu.VMEM((images, tokens, heads_width), bf16),
        hidden=pltpu.VMEM((images, tokens, units), bf16),
        near_out0=pltpu.VMEM((half, tokens, width), bf16),
        near_in0=pltpu.VMEM((half, tokens, width), bf16),
        far_out0=pltpu.VMEM((half, tokens, width), bf16),
        far_in0=pltpu.VMEM((half, tokens, width), bf16),
        near_out1=pltpu.VMEM((blocks, half, tokens, block), bf16),
        near_in1=pltpu.VMEM((blocks, half, tokens, block), bf16),
        far_out1=pltpu.VMEM((blocks, half, tokens, block), bf16),
        far_in1=pltpu.VMEM((blocks, half, tokens, block), bf16),
        logits_v=pltpu.VMEM((images, tokens, vocab), bf16),
        z_recv=dma((chunks, 2, outer)),
        up_send=dma((chunks, 2, outer)),
        down_send=dma((chunks, 2, outer)),
        y_recv=dma((chunks, outer)),
        y_send=dma((chunks, outer)),
        load=dma((len(INPUTS),)),
        store=dma((images + 1,)),
        near0=dma((2, half)),
        far0=dma((2, half)),
        near1=dma((2, blocks, 3, half)),
        far1=dma((2, blocks, 3, half)),
        swap2=dma((2, half)),
        swap3=dma((2, half)),
    )


class Bag:
    def __init__(self, names, values):
        self.__dict__.update(zip(names, values))


def step_kernel(dims, *refs):
    outer, rows, images, tokens = dims.outer, dims.rows, dims.images, dims.tokens
    width, heads_width, units = dims.width, dims.heads_width, dims.units
    head_total, head_size = dims.heads, dims.heads_width // dims.heads
    half, blocks, vocab = dims.half, dims.blocks, dims.vocab
    block = width // blocks
    given = Given(*refs[: len(INPUTS)])
    logits_hbm, canvas_hbm = refs[len(INPUTS) : len(INPUTS) + 2]
    v = Bag(list(scratch_shapes(dims)), refs[len(INPUTS) + 2 :])

    relay = Relay(
        outer, rows, (v.w_qkv, v.w_out, v.w_up, v.w_down), dims.parts, dims.early,
        (v.z_recv, v.up_send, v.down_send, v.y_recv, v.y_send),
    )
    dp, t, o, p = relay.dp, relay.t, relay.o, relay.p
    core = lax.rem(t, 2)
    near_t = t + 1 - 2 * core
    far_t = lax.rem(t + 2, 4)
    own_rows = pl.ds(pl.multiple_of(dp * rows, rows), rows)

    loads = {}

    spot = Given(*range(len(INPUTS)))

    def load(index, target):
        loads[index] = pltpu.make_async_copy(given[index], target, v.load.at[index])
        loads[index].start()

    load(spot.qkv, v.w_qkv.at[:, own_rows])
    load(spot.out, v.w_out.at[own_rows])
    load(spot.up, v.w_up.at[own_rows])
    load(spot.codes, v.s_codes)
    load(spot.ids, v.s_ids)
    load(spot.grow, v.s_grow)
    load(spot.summed, v.s_summed)
    load(spot.lift, v.s_lift)
    load(spot.offset, v.s_offset)
    load(spot.factors, v.s_factors)
    load(spot.down, v.w_down.at[own_rows])
    load(spot.keys, v.s_keys)
    load(spot.values, v.s_values)
    load(spot.head_factors, v.s_head_factors)
    load(spot.vocab, v.s_vocab)

    barrier = pltpu.get_barrier_semaphore()

    def greet(target):
        pl.semaphore_signal(barrier, inc=1, device_id=target, device_id_type=MESH)

    greet((o * 2 + 1 - p, t))
    greet((dp, near_t))
    greet((dp, far_t))
    pl.when(o > 0)(lambda: greet((dp - 2, t)))
    pl.when(o < outer - 1)(lambda: greet((dp + 2, t)))
    ends = jnp.where(o > 0, 1, 0) + jnp.where(o < outer - 1, 1, 0)
    pl.semaphore_wait(barrier, 3 + ends)

    chunks = [
        [(matrix, part) for part in range(count)] for matrix, count in enumerate(dims.parts)
    ]
    first = chunks[QKV] + chunks[OUT]

    def begin_y(group):
        for chunk in group:
            if relay.crosses_early(chunk):
                relay.start_y(chunk)

    loads[spot.qkv].wait()
    begin_y(chunks[QKV])
    relay.own_z(chunks[QKV])
    relay.own_y(chunks[QKV])
    loads[spot.out].wait()
    begin_y(chunks[OUT])
    relay.own_z(chunks[OUT])

    loads[spot.codes].wait()
    channels = dims.channels

    def split_codes(tile):
        cols = pl.ds(pl.multiple_of(tile * 512, 512), 512)
        left = v.s_codes[:, cols]
        for part in range(3):
            piece = left.astype(bf16)
            v.code_parts[part * channels : (part + 1) * channels, cols] = piece
            left = left - piece.astype(f32)

    with jax.named_scope("split_codes"):
        loop(dims.codes // 512, split_codes)
    for name in (spot.ids, spot.grow, spot.summed, spot.lift, spot.offset, spot.factors):
        loads[name].wait()

    inner = jnp.logical_and(o > 0, o < outer - 1)

    def inside(when, act):
        pl.when(jnp.logical_and(inner, when))(act)

    def at_end(when, act):
        pl.when(jnp.logical_and(jnp.logical_not(inner), when))(act)

    def image_of(slot):
        return lax.rem(half * (1 - core) + slot, images)

    prev = dims.prev
    vocab_tile = 1024

    def factor(row, image, cols=slice(None)):
        return v.s_factors[row, pl.ds(image, 1), cols]

    def embed(slot):
        image = image_of(slot)
        ids_row = v.s_ids[pl.ds(image, 1), :].astype(f32)
        same = lax.broadcasted_iota(jnp.int32, (prev, prev), 0) == lax.broadcasted_iota(
            jnp.int32, (prev, prev), 1
        )
        ids = jnp.sum(jnp.where(same, ids_row, 0.0), axis=1, keepdims=True)

        def codes_tile(tile, total):
            place = lax.broadcasted_iota(jnp.int32, (prev, vocab_tile), 1).astype(f32) + (
                tile * vocab_tile
            ).astype(f32)
            onehot = jnp.where(ids == place, 1.0, 0.0).astype(bf16)
            cols = pl.ds(pl.multiple_of(tile * vocab_tile, vocab_tile), vocab_tile)
            return total + dot_t(v.code_parts[:, cols], onehot)

        parts = lax.fori_loop(
            0, dims.codes // vocab_tile, codes_tile, jnp.zeros((3 * channels, prev), f32)
        )
        embedded = parts[:channels] + parts[channels : 2 * channels] + parts[2 * channels :]
        grown = lax.dot_general(
            embedded, v.s_grow[...], (((1,), (1,)), ((), ())), precision=highest,
            preferred_element_type=f32,
        )
        canvas = v.s_summed[image] + grown
        v.canvas_v[image] = canvas
        stream = (
            jnp.dot(canvas.T, v.s_lift[...], precision=highest, preferred_element_type=f32)
            + v.s_offset[...]
        )
        v.normed[slot] = modulate(stream, factor(2, image), factor(4, image)).astype(bf16)

        @pl.when(slot >= half)
        def _():
            v.stream[slot - half] = stream

        for head in range(head_total):
            low = head * head_size
            high = low + head_size
            old = slice(tokens, tokens + dims.cache)
            v.all_keys[image, head, old, :] = unit(
                v.s_keys[image, :, low:high].astype(f32)
            ).astype(bf16)
            v.all_values[image, head] = jnp.ones((tokens + dims.cache, 128), bf16)
            v.all_values[image, head, old, :head_size] = v.s_values[image, :, low:high]

        @pl.when(slot == 1)
        def _():
            relay.cross_z(first)
            relay.steps(first, 0)
            begin_y(chunks[UP])

        @pl.when(slot == 2)
        def _():
            relay.steps(first, 1)
            relay.own_z(chunks[UP])

        @pl.when(slot == 3)
        def _():
            relay.steps(first, 2)
            if not relay.crosses_early((OUT, 0)):
                relay.own_y(chunks[OUT])
                relay.cross_rest(chunks[OUT])
            relay.own_y(chunks[UP])
            begin_y(chunks[DOWN])

    loads[spot.keys].wait()
    loads[spot.values].wait()
    loads[spot.up].wait()
    loads[spot.down].wait()
    loop(images, embed, "embed")
    canvas_out = pltpu.make_async_copy(v.canvas_v, canvas_hbm, v.store.at[images])
    canvas_out.start()
    relay.cross_z(chunks[UP])
    relay.wait_y_all(chunks[QKV])

    def near_copy(name, sems, index):
        source, target = name
        return pltpu.make_async_remote_copy(
            src_ref=source, dst_ref=target, send_sem=sems.at[(0, *index)],
            recv_sem=sems.at[(1, *index)], device_id=(dp, near_t), device_id_type=MESH,
        )

    def far_copy(name, sems, index):
        source, target = name
        return pltpu.make_async_remote_copy(
            src_ref=source, dst_ref=target, send_sem=sems.at[(0, *index)],
            recv_sem=sems.at[(1, *index)], device_id=(dp, far_t), device_id_type=MESH,
        )

    def near0(j):
        return near_copy((v.near_out0.at[j], v.near_in0.at[j]), v.near0, (j,))

    def far0(j):
        return far_copy((v.far_out0.at[j], v.far_in0.at[j]), v.far0, (j,))

    def near1(n, j, piece, turn):
        name = (v.near_out1.at[n, j, :, piece], v.near_in1.at[n, j, :, piece])
        return near_copy(name, v.near1, (n, turn, j))

    def far1(n, j, piece, turn):
        name = (v.far_out1.at[n, j, :, piece], v.far_in1.at[n, j, :, piece])
        return far_copy(name, v.far1, (n, turn, j))

    def swap2(j):
        return near_copy((v.normed2.at[half + j], v.normed2.at[j]), v.swap2, (j,))

    def swap3(j):
        return near_copy((v.normed3.at[half + j], v.normed3.at[j]), v.swap3, (j,))

    def attend(turn):
        slot = slot_of(turn)
        image = image_of(slot)

        @pl.when(turn == 2)
        def _():
            inside(True, lambda: relay.steps(chunks[UP], 1))
            relay.own_z(chunks[DOWN])
            relay.cross_z(chunks[DOWN])
            inside(True, lambda: relay.own_y(chunks[DOWN]))

        def project(tile):
            cols = pl.ds(pl.multiple_of(tile * heads_width, heads_width), heads_width)
            v.projected[:, cols] = dot(v.normed[slot], v.w_qkv[tile])

        loop(3, project)
        for head in range(head_total):
            low = head * head_size
            high = low + head_size
            query = (unit(v.projected[:, low:high]) * given.sharp[0, head]).astype(bf16)
            key_new = unit(v.projected[:, heads_width + low : heads_width + high]).astype(bf16)
            value_new = v.projected[:, 2 * heads_width + low : 2 * heads_width + high].astype(bf16)
            keys, values = v.all_keys.at[image, head], v.all_values.at[image, head]
            keys[:tokens, :] = key_new
            values[:tokens, :head_size] = value_new
            scores = dot_t(query, keys[...])
            weights = jnp.exp(scores - jnp.max(scores, axis=-1, keepdims=True)).astype(bf16)
            mixed = dot(weights, values[...])
            total = mixed[:, head_size : head_size + 1]
            v.attended[slot, :, low:high] = (mixed[:, :head_size] / total).astype(bf16)
            if head == 1:
                at_end(turn == 1, lambda: relay.steps(chunks[UP], 0))
                at_end(turn == 3, lambda: relay.steps(chunks[UP], 1))

        inside(turn == 0, lambda: relay.steps(chunks[UP], 0))

        @pl.when(turn == 1)
        def _():
            relay.wait_y_all(chunks[OUT])

        @pl.when(turn > 0)
        def _():
            loop(jnp.where(turn == 1, 2, 1), lambda back: project_out(turn - jnp.where(turn == 1, 1, 0) + back))

    def slot_of(turn):
        return turn // 2 + half * lax.rem(turn, 2)

    def project_out(turn):
        slot = slot_of(turn)
        image = image_of(slot)

        @pl.when(slot >= half)
        def _():
            near0(slot - half).wait_recv()

        def out_tile(tile):
            cols = pl.ds(pl.multiple_of(tile * block, block), block)
            partial = dot_t(v.attended[slot], v.w_out[cols, :])

            @pl.when(slot < half)
            def _():
                v.near_out0[slot, :, cols] = partial.astype(bf16)

            @pl.when(slot >= half)
            def _():
                pair = partial + v.near_in0[slot - half, :, cols].astype(f32)
                v.far_out0[slot - half, :, cols] = pair.astype(bf16)
                v.stream[slot - half, :, cols] += factor(0, image, cols) * pair

        loop(blocks, out_tile)
        pl.when(slot < half)(lambda: near0(slot).start())
        pl.when(slot >= half)(lambda: far0(slot - half).start())

    loop(images, attend, "attend")

    def second_norm(j):
        image = image_of(half + j)
        v.gain[j] = factor(1, image)
        far0(j).wait_recv()
        stream = v.stream[j] + factor(0, image) * v.far_in0[j].astype(f32)
        v.stream[j] = stream
        v.normed2[half + j] = modulate(stream, factor(3, image), factor(5, image)).astype(bf16)
        swap2(j).start()

    def second_norms(j):
        second_norm(j)

        @pl.when(j == 0)
        def _():
            relay.steps(chunks[UP], 2)
            at_end(True, lambda: relay.own_y(chunks[DOWN]))
            inside(True, lambda: relay.steps(chunks[DOWN], 0))

    loop(half, second_norms, "second_norm")
    relay.wait_y_all(chunks[UP])

    unit_tile = 512

    def lift_units(turn):
        slot = turn // 2 + half * (1 - lax.rem(turn, 2))
        pl.when(slot < half)(lambda: swap2(slot).wait_recv())

        def tile_units(tile):
            cols = pl.ds(pl.multiple_of(tile * unit_tile, unit_tile), unit_tile)
            lifted = dot(v.normed2[slot], v.w_up[:, cols])
            v.hidden[slot, :, cols] = jax.nn.gelu(lifted, approximate=True).astype(bf16)

        loop(units // unit_tile, tile_units)
        at_end(turn == 1, lambda: relay.steps(chunks[DOWN], 0))
        inside(turn == 1, lambda: relay.steps(chunks[DOWN], 1))

    loop(images, lift_units, "lift_units")

    both = jnp.minimum(o, outer - 1 - o)
    sign = jnp.where(o < outer - 1 - o, 1, -1)

    def block_of(n):
        if blocks != outer:
            return n
        distance = (n + 1) // 2
        beside = o + distance * (1 - 2 * lax.rem(n, 2))
        beyond = o + sign * (n - both)
        return jnp.where(n <= 2 * both, beside, beyond)

    if blocks != outer:
        at_end(True, lambda: relay.steps(chunks[DOWN], 1))
        relay.steps(chunks[DOWN], 2)
        relay.wait_y_all(chunks[DOWN])

    def wait_down(n, parts):
        if blocks == outer:
            for chunk in parts:
                if not relay.crosses_early(chunk):
                    relay.wait_y(chunk, block_of(n))

    def down_piece(n, low, size):
        start = block_of(n) * block + low
        cols = pl.ds(pl.multiple_of(start, 128), size)
        piece = slice(low, low + size)
        turn = low // size

        def theirs(j):
            v.near_out1[n, j, :, piece] = dot_t(v.hidden[j], v.w_down[cols, :]).astype(bf16)
            near1(n, j, piece, turn).start()

        loop(half, theirs)

        def ours(j):
            partial = dot_t(v.hidden[half + j], v.w_down[cols, :])
            near1(n, j, piece, turn).wait_recv()
            pair = partial + v.near_in1[n, j, :, piece].astype(f32)
            v.far_out1[n, j, :, piece] = pair.astype(bf16)
            far1(n, j, piece, turn).start()
            v.stream[j, :, cols] += v.gain[j, :, cols] * pair

        loop(half, ours)

    def add_far(n, j, low, size):
        start = block_of(n) * block + low
        cols = pl.ds(pl.multiple_of(start, 128), size)
        piece = slice(low, low + size)
        far1(n, j, piece, low // size).wait_recv()
        v.stream[j, :, cols] += v.gain[j, :, cols] * v.far_in1[n, j, :, piece].astype(f32)

    def down_block(n):
        if blocks == outer:
            at_end(n == 1, lambda: relay.steps(chunks[DOWN], 1))
            pl.when(n == 2)(lambda: relay.steps(chunks[DOWN], 2))
        with jax.named_scope("wait_down"):
            wait_down(n, chunks[DOWN])
        down_piece(n, 0, block)

        @pl.when(n > 0)
        def _():
            loop(half, lambda j: add_far(n - 1, j, 0, block))

    loop(blocks - 1, down_block, "down_block")
    end = blocks - 1
    part = block // 3
    most = 2 * len(chunks[DOWN]) // 3
    with jax.named_scope("last_wait"):
        wait_down(end, chunks[DOWN][:most])
    down_piece(end, 0, part)
    down_piece(end, 2 * part, part)
    loop(half, lambda j: add_far(end - 1, j, 0, block))
    with jax.named_scope("last_wait"):
        wait_down(end, chunks[DOWN][most:])
    down_piece(end, part, part)
    with jax.named_scope("drain"):
        relay.drain()
    loads[spot.head_factors].wait()
    loads[spot.vocab].wait()

    def last_norm(j):
        image = image_of(half + j)
        for low in (0, 2 * part, part):
            add_far(end, j, low, part)
        factors = v.s_head_factors.at[image]
        v.normed3[half + j] = modulate(
            v.stream[j], factors[0:1, :], factors[1:2, :]
        ).astype(bf16)
        swap3(j).start()

    loop(half, last_norm, "last_norm")

    def logits_out(image):
        return pltpu.make_async_copy(
            v.logits_v.at[image], logits_hbm.at[image], v.store.at[image]
        )

    def give_logits(turn):
        slot = lax.rem(turn + half, images)
        image = image_of(slot)
        pl.when(slot < half)(lambda: swap3(slot).wait_recv())
        v.logits_v[image] = dot(v.normed3[slot], v.s_vocab[...]).astype(bf16)
        logits_out(image).start()

    loop(images, give_logits, "give_logits")

    def finish(j):
        near0(j).wait_send()
        far0(j).wait_send()
        swap2(j).wait_send()
        swap3(j).wait_send()

        def block_done(n):
            near1(n, j, slice(0, block), 0).wait_send()
            far1(n, j, slice(0, block), 0).wait_send()

        loop(blocks - 1, block_done)
        for low in (0, part, 2 * part):
            piece = slice(low, low + part)
            near1(end, j, piece, low // part).wait_send()
            far1(end, j, piece, low // part).wait_send()

    loop(half, finish)
    loop(images, lambda image: logits_out(image).wait())
    canvas_out.wait()


def local(
    dp_total, tensor_total, ids, codes, summed, lift, offset, factors, sharp, qkv, out, up, down,
    keys, values, head_factors, vocab,
):
    images, prev = ids.shape
    tokens, width = offset.shape
    rows = qkv.shape[1]
    outer = dp_total // 2
    group = 1
    while (2 * rows * group) % 128:
        group *= 2
    heads_width = out.shape[1]
    assert tensor_total == 4 and images % 2 == 0 and dp_total % 2 == 0
    down_parts = 6 if rows % 96 == 0 else 3
    dims = SimpleNamespace(
        outer=outer, rows=rows, images=images, tokens=tokens, width=width,
        heads_width=heads_width, heads=sharp.shape[1], units=up.shape[2],
        prev=prev, channels=codes.shape[1], codes=codes.shape[0],
        vocab=vocab.shape[1], cache=keys.shape[2], half=images // 2,
        blocks=outer // group, parts=(3, 1, 3, down_parts), early=EARLY,
    )
    grow = interp_matrix(SIDE, PREV)
    grow = jnp.asarray(np.kron(grow, grow), f32)
    given = (
        ids, codes.T, summed.swapaxes(1, 2), lift, offset, factors[0].swapaxes(0, 1), sharp,
        qkv[0].swapaxes(0, 1), out[0].T, up[0], down[0].T, keys[0], values[0],
        head_factors, vocab, grow,
    )
    anywhere = pl.BlockSpec(memory_space=pl.ANY)
    specs = [anywhere] * len(INPUTS)
    specs[Given(*range(len(INPUTS))).sharp] = pl.BlockSpec(memory_space=pltpu.SMEM)
    logits, canvas = pl.pallas_call(
        functools.partial(step_kernel, dims),
        out_shape=(
            jax.ShapeDtypeStruct((images, tokens, vocab.shape[1]), bf16),
            jax.ShapeDtypeStruct((images, summed.shape[2], tokens), f32),
        ),
        in_specs=specs,
        out_specs=(anywhere, anywhere),
        scratch_shapes=list(scratch_shapes(dims).values()),
        compiler_params=pltpu.CompilerParams(
            collective_id=0, has_side_effects=True, vmem_limit_bytes=67043328
        ),
        name="step",
    )(*given)
    return logits, canvas.swapaxes(1, 2)


def solution(mesh):
    placed = (
        P("dp", None),
        P(),
        P("dp", None, None),
        P(),
        P(),
        P(None, "dp", None, None),
        P(None, "tensor"),
        P(None, "dp", None, "tensor"),
        P(None, "tensor", "dp"),
        P(None, "dp", "tensor"),
        P(None, "tensor", "dp"),
        P(None, "dp", None, "tensor"),
        P(None, "dp", None, "tensor"),
        P("dp", None, None),
        P(None, "tensor"),
    )
    return jax.shard_map(
        functools.partial(local, mesh.shape["dp"], mesh.shape["tensor"]),
        mesh=mesh,
        in_specs=placed,
        out_specs=(P("dp", None, "tensor"), P("dp", None, None)),
        check_vma=False,
    )
```

profile of v0, /device:TPU:0, one launch (start us, length us, event | category | flops | bytes accessed | tf_op | source)
XLA Modules:
  0.0 175.0 jit_solution(2040856844594328114)
XLA Ops:
  0.6 170.6 %step.1 = (bf16[4,256,1024]{2,1,0:T(8,128)(2,1)}, f32[4,32,256]{2,1,0:T(8,128)}) custom-call(s32[4,169]{1,0:T(4,128)} %refs_0_.1, f32[32,4096]{1,0:T(8,128)} %bitcast.22, f32[4,32,256]{2,1,0:T(8,128)} %bitcast.26, f32[32,1536]{1,0:T(8,128)} %refs_3_.1, f32[256,1536]{1,0:T(8,128)} %refs_4_.1, f32[6,4,1536]{2,1,0:T(4,128)} %bitcast.24, f32[1,4]{1,0:T(1,128)} %refs_6_.1, ...), custom_call_target="tpu_custom_call" | custom-call | tf_op jit(solution)/shard_map/step/pallas_call | solution.py:805
  171.2 0.0 copy-start
  171.2 3.1 %copy.20 = bf16[4,256,1024]{2,1,0:T(8,128)(2,1)} copy(bf16[4,256,1024]{2,1,0:T(8,128)(2,1)} %get-tuple-element.8) | data formatting | bytes 4194304
  174.3 0.0 copy-done
  174.3 0.7 copy.21
Async XLA Ops:
  171.2 3.1 %copy-start = (f32[4,32,256]{2,1,0:T(8,128)S(1)}, f32[4,32,256]{2,1,0:T(8,128)}, u32[]{:S(2)}) copy-start(f32[4,32,256]{2,1,0:T(8,128)} %get-tuple-element.5) | copy-start | bytes 393220
where the time goes:
time: 175 us
  Pallas kernels  171 us (98%)
  local copies, waits for them, and re-layouts  3.77 us (2%)
    pallas_call x1, Pallas kernels, local(): pl.pallas_call(functools.partial(step_kernel, dims), out_shape=(jax.Shape...  171 us
    unnamed x4, local copies, waits for them, and re-layouts  3.77 us

commit v1 on v0

--- a/solution.py
+++ b/solution.py
@@ -71,11 +71,32 @@
         self.early = early
         self.dp, self.t = lax.axis_index("dp"), lax.axis_index("tensor")
         self.o, self.p = self.dp // 2, lax.rem(self.dp, 2)
-        self.z_recv, self.up_send, self.down_send, self.y_recv, self.y_send = sems
-        self.number = {}
+        self.z_recv, self.z_send, self.y_recv, self.y_each, self.y_send = sems
+        self.number, self.lane = {}, {}
         for matrix, count in enumerate(parts):
             for part in range(count):
                 self.number[(matrix, part)] = len(self.number)
+        for chunk in self.number:
+            self.lane[chunk, 0] = len(self.lane)
+        for chunk in early:
+            self.lane[chunk, 1] = len(self.lane)
+
+    def span(self, chunk, copies):
+        matrix, part = chunk
+        if matrix == QKV:
+            return self.buffers[matrix].at[part, pl.ds(0, copies * self.rows)]
+        return self.buffers[matrix].at[pl.ds(0, copies * (self.rows // self.parts[matrix]))]
+
+    def wait(self, ref, send=None, recv=None):
+        copy = pltpu.make_async_remote_copy(
+            src_ref=ref, dst_ref=ref,
+            send_sem=recv if send is None else send, recv_sem=send if recv is None else recv,
+            device_id=(self.o * 2 + 1 - self.p, self.t), device_id_type=MESH,
+        )
+        if send is None:
+            copy.wait_recv()
+        else:
+            copy.wait_send()
 
     def ref(self, chunk, o, plane):
         matrix, part = chunk
@@ -91,16 +112,21 @@
         start = (o * 2 + p) * self.rows + part * rows
         return self.buffers[matrix].at[pl.ds(pl.multiple_of(start, rows), rows)]
 
+    def y_arrival(self, chunk, src):
+        if chunk[0] == DOWN and not self.crosses_early(chunk):
+            return self.y_each.at[chunk[1], src]
+        return self.y_recv.at[self.number[chunk]]
+
     def copy(self, way, chunk, src, plane):
         ref = self.ref(chunk, src, plane)
-        number = self.number[chunk]
         if way == "y":
             target = self.o * 2 + 1 - self.p
-            send, recv = self.y_send.at[number, src], self.y_recv.at[number, src]
+            send, recv = self.y_send.at[self.number[chunk]], self.y_arrival(chunk, src)
         else:
+            lane = self.lane[chunk, plane]
             target = self.dp + 2 if way == "up" else self.dp - 2
-            sends = self.up_send if way == "up" else self.down_send
-            send, recv = sends.at[number, plane, src], self.z_recv.at[number, plane, src]
+            send = self.z_send.at[lane]
+            recv = self.z_recv.at[lane, src if way == "up" else src - 1]
         return pltpu.make_async_remote_copy(
             src_ref=ref, dst_ref=ref, send_sem=send, recv_sem=recv,
             device_id=(target, self.t), device_id_type=MESH,
@@ -148,49 +174,42 @@
         loop(self.outer, rest)
 
     def wait_y(self, chunk, src):
-        ref = self.ref(chunk, src, 1)
-        number = self.number[chunk]
-        pltpu.make_async_remote_copy(
-            src_ref=ref, dst_ref=ref, send_sem=self.y_send.at[number, src],
-            recv_sem=self.y_recv.at[number, src],
-            device_id=(self.o * 2 + 1 - self.p, self.t), device_id_type=MESH,
-        ).wait_recv()
+        self.wait(self.ref(chunk, src, 1), recv=self.y_arrival(chunk, src))
 
     def wait_y_all(self, chunks):
         with jax.named_scope("wait_y"):
-            self.wait_y_each(chunks)
-
-    def wait_y_each(self, chunks):
-        for chunk in chunks:
-            if not self.crosses_early(chunk):
-                loop(self.outer, lambda src: self.wait_y(chunk, src))
+            for chunk in chunks:
+                if self.crosses_early(chunk):
+                    continue
+                if chunk[0] == DOWN:
+                    loop(self.outer, lambda src: self.wait_y(chunk, src))
+                else:
+                    self.wait(self.span(chunk, self.outer), recv=self.y_arrival(chunk, 0))
 
     def step(self, chunks, s):
+        below = ("up", self.o - s, self.o >= s)
+        above = ("down", self.o + s, self.o + s < self.outer)
         with jax.named_scope("relay"):
-            self.step_inner(chunks, s)
-
-    def step_inner(self, chunks, s):
-        for chunk in chunks:
-            early = self.crosses_early(chunk)
+            if chunks[0][0] == DOWN:
+                for side in (below, above):
+                    for chunk in chunks:
+                        self.pass_on(chunk, *side)
+            else:
+                for chunk in chunks:
+                    for side in (below, above):
+                        self.pass_on(chunk, *side)
+
+    def pass_on(self, chunk, way, src, there):
+        early = self.crosses_early(chunk)
+
+        @pl.when(there)
+        def _():
             for plane in (0, 1) if early else (0,):
-                for way, src, there in (
-                    ("up", self.o - s, self.o >= s),
-                    ("down", self.o + s, self.o + s < self.outer),
-                ):
-
-                    @pl.when(there)
-                    def _():
-                        ref = self.ref(chunk, src, plane)
-                        number = self.number[chunk]
-                        pltpu.make_async_remote_copy(
-                            src_ref=ref, dst_ref=ref,
-                            send_sem=self.up_send.at[number, plane, src],
-                            recv_sem=self.z_recv.at[number, plane, src],
-                            device_id=(self.o * 2 + 1 - self.p, self.t), device_id_type=MESH,
-                        ).wait_recv()
-                        self.sends(way, chunk, src, plane, lambda copy: copy.start())
-                        if not early and chunk[0] != OUT:
-                            self.sends("y", chunk, src, plane, lambda copy: copy.start())
+                arrived = self.z_recv.at[self.lane[chunk, plane], src if way == "up" else src - 1]
+                self.wait(self.ref(chunk, src, plane), recv=arrived)
+                self.sends(way, chunk, src, plane, lambda copy: copy.start())
+                if not early and chunk[0] != OUT:
+                    self.sends("y", chunk, src, plane, lambda copy: copy.start())
 
     def steps(self, chunks, third):
         span = self.outer - 1
@@ -201,28 +220,21 @@
             loop(high - low, lambda index: self.step(chunks, low + index))
 
     def drain(self):
-        def done(copy):
-            copy.wait_send()
-
-        for chunk in self.number:
-            early = self.crosses_early(chunk)
-            for plane in (0, 1) if early else (0,):
-
-                def sent(src):
-                    @pl.when(src <= self.o)
-                    def _():
-                        self.sends("up", chunk, src, plane, done)
-
-                    @pl.when(src >= self.o)
-                    def _():
-                        self.sends("down", chunk, src, plane, done)
-
-                    if not early:
-                        self.sends("y", chunk, src, plane, done)
-
-                loop(self.outer, sent)
-            if early:
-                self.start_y(chunk, done)
+        inner = jnp.logical_and(self.o > 0, self.o < self.outer - 1)
+        for (chunk, plane), lane in self.lane.items():
+            sent = self.z_send.at[lane]
+
+            @pl.when(inner)
+            def _():
+                self.wait(self.span(chunk, self.outer + 1), send=sent)
+
+            @pl.when(jnp.logical_not(inner))
+            def _():
+                self.wait(self.span(chunk, 1), send=sent)
+
+        for chunk, number in self.number.items():
+            copies = 1 if self.crosses_early(chunk) else self.outer
+            self.wait(self.span(chunk, copies), send=self.y_send.at[number])
 
 
 class Given(NamedTuple):
@@ -253,6 +265,7 @@
     prev, channels, vocab, codes = dims.prev, dims.channels, dims.vocab, dims.codes
     cache, half, blocks = dims.cache, dims.half, dims.blocks
     chunks = sum(dims.parts)
+    lanes = chunks + len(dims.early)
     dma = pltpu.SemaphoreType.DMA
     block = width // blocks
     return dict(
@@ -292,19 +305,20 @@
         far_out1=pltpu.VMEM((blocks, half, tokens, block), bf16),
         far_in1=pltpu.VMEM((blocks, half, tokens, block), bf16),
         logits_v=pltpu.VMEM((images, tokens, vocab), bf16),
-        z_recv=dma((chunks, 2, outer)),
-        up_send=dma((chunks, 2, outer)),
-        down_send=dma((chunks, 2, outer)),
-        y_recv=dma((chunks, outer)),
-        y_send=dma((chunks, outer)),
+        z_recv=dma((lanes, outer - 1)),
+        z_send=dma((lanes,)),
+        y_recv=dma((chunks,)),
+        y_each=dma((dims.parts[DOWN], outer)),
+        y_send=dma((chunks,)),
         load=dma((len(INPUTS),)),
         store=dma((images + 1,)),
-        near0=dma((2, half)),
-        far0=dma((2, half)),
-        near1=dma((2, blocks, 3, half)),
-        far1=dma((2, blocks, 3, half)),
-        swap2=dma((2, half)),
-        swap3=dma((2, half)),
+        sent=dma((6,)),
+        near0=dma((half,)),
+        far0=dma((half,)),
+        near1=dma((blocks + 2, half)),
+        far1=dma((blocks + 2, half)),
+        swap2=dma((half,)),
+        swap3=dma((half,)),
     )
 
 
@@ -325,7 +339,7 @@
 
     relay = Relay(
         outer, rows, (v.w_qkv, v.w_out, v.w_up, v.w_down), dims.parts, dims.early,
-        (v.z_recv, v.up_send, v.down_send, v.y_recv, v.y_send),
+        (v.z_recv, v.z_send, v.y_recv, v.y_each, v.y_send),
     )
     dp, t, o, p = relay.dp, relay.t, relay.o, relay.p
     core = lax.rem(t, 2)
@@ -497,39 +511,31 @@
     relay.cross_z(chunks[UP])
     relay.wait_y_all(chunks[QKV])
 
-    def near_copy(name, sems, index):
-        source, target = name
+    def pair_copy(source, target, lane, recv, t_other):
         return pltpu.make_async_remote_copy(
-            src_ref=source, dst_ref=target, send_sem=sems.at[(0, *index)],
-            recv_sem=sems.at[(1, *index)], device_id=(dp, near_t), device_id_type=MESH,
+            src_ref=source, dst_ref=target, send_sem=v.sent.at[lane], recv_sem=recv,
+            device_id=(dp, t_other), device_id_type=MESH,
         )
 
-    def far_copy(name, sems, index):
-        source, target = name
-        return pltpu.make_async_remote_copy(
-            src_ref=source, dst_ref=target, send_sem=sems.at[(0, *index)],
-            recv_sem=sems.at[(1, *index)], device_id=(dp, far_t), device_id_type=MESH,
-        )
-
     def near0(j):
-        return near_copy((v.near_out0.at[j], v.near_in0.at[j]), v.near0, (j,))
+        return pair_copy(v.near_out0.at[j], v.near_in0.at[j], 0, v.near0.at[j], near_t)
 
     def far0(j):
-        return far_copy((v.far_out0.at[j], v.far_in0.at[j]), v.far0, (j,))
+        return pair_copy(v.far_out0.at[j], v.far_in0.at[j], 1, v.far0.at[j], far_t)
 
     def near1(n, j, piece, turn):
-        name = (v.near_out1.at[n, j, :, piece], v.near_in1.at[n, j, :, piece])
-        return near_copy(name, v.near1, (n, turn, j))
+        source, target = v.near_out1.at[n, j, :, piece], v.near_in1.at[n, j, :, piece]
+        return pair_copy(source, target, 2, v.near1.at[n + turn, j], near_t)
 
     def far1(n, j, piece, turn):
-        name = (v.far_out1.at[n, j, :, piece], v.far_in1.at[n, j, :, piece])
-        return far_copy(name, v.far1, (n, turn, j))
+        source, target = v.far_out1.at[n, j, :, piece], v.far_in1.at[n, j, :, piece]
+        return pair_copy(source, target, 3, v.far1.at[n + turn, j], far_t)
 
     def swap2(j):
-        return near_copy((v.normed2.at[half + j], v.normed2.at[j]), v.swap2, (j,))
+        return pair_copy(v.normed2.at[half + j], v.normed2.at[j], 4, v.swap2.at[j], near_t)
 
     def swap3(j):
-        return near_copy((v.normed3.at[half + j], v.normed3.at[j]), v.swap3, (j,))
+        return pair_copy(v.normed3.at[half + j], v.normed3.at[j], 5, v.swap3.at[j], near_t)
 
     def attend(turn):
         slot = slot_of(turn)
@@ -695,30 +701,37 @@
         far1(n, j, piece, low // size).wait_recv()
         v.stream[j, :, cols] += v.gain[j, :, cols] * v.far_in1[n, j, :, piece].astype(f32)
 
+    most = 2 * len(chunks[DOWN]) // 3
+    front, back = chunks[DOWN][:most], chunks[DOWN][most:]
+    end = blocks - 1
+    part = block // 3
+
+    def down_relays(n, group):
+        if blocks == outer:
+            at_end(n == 1, lambda: relay.steps(group, 1))
+            pl.when(n == 2)(lambda: relay.steps(group, 2))
+
     def down_block(n):
-        if blocks == outer:
-            at_end(n == 1, lambda: relay.steps(chunks[DOWN], 1))
-            pl.when(n == 2)(lambda: relay.steps(chunks[DOWN], 2))
+        down_relays(n, front)
         with jax.named_scope("wait_down"):
             wait_down(n, chunks[DOWN])
         down_piece(n, 0, block)
-
-        @pl.when(n > 0)
-        def _():
-            loop(half, lambda j: add_far(n - 1, j, 0, block))
-
-    loop(blocks - 1, down_block, "down_block")
-    end = blocks - 1
-    part = block // 3
-    most = 2 * len(chunks[DOWN]) // 3
+        down_relays(n, back)
+
+        @pl.when(n > 1)
+        def _():
+            loop(half, lambda j: add_far(n - 2, j, 0, block))
+
+    loop(end, down_block, "down_block")
     with jax.named_scope("last_wait"):
-        wait_down(end, chunks[DOWN][:most])
+        wait_down(end, front)
     down_piece(end, 0, part)
     down_piece(end, 2 * part, part)
+    with jax.named_scope("last_wait"):
+        wait_down(end, back)
+    down_piece(end, part, part)
+    loop(half, lambda j: add_far(end - 2, j, 0, block))
     loop(half, lambda j: add_far(end - 1, j, 0, block))
-    with jax.named_scope("last_wait"):
-        wait_down(end, chunks[DOWN][most:])
-    down_piece(end, part, part)
     with jax.named_scope("drain"):
         relay.drain()
     loads[spot.head_factors].wait()
@@ -750,23 +763,13 @@
 
     loop(images, give_logits, "give_logits")
 
-    def finish(j):
-        near0(j).wait_send()
-        far0(j).wait_send()
-        swap2(j).wait_send()
-        swap3(j).wait_send()
-
-        def block_done(n):
-            near1(n, j, slice(0, block), 0).wait_send()
-            far1(n, j, slice(0, block), 0).wait_send()
-
-        loop(blocks - 1, block_done)
-        for low in (0, part, 2 * part):
-            piece = slice(low, low + part)
-            near1(end, j, piece, low // part).wait_send()
-            far1(end, j, piece, low // part).wait_send()
-
-    loop(half, finish)
+    for lane, source in enumerate(
+        (
+            v.near_out0, v.far_out0, v.near_out1, v.far_out1,
+            v.normed2.at[pl.ds(half, half)], v.normed3.at[pl.ds(half, half)],
+        )
+    ):
+        relay.wait(source, send=v.sent.at[lane])
     loop(images, lambda image: logits_out(image).wait())
     canvas_out.wait()
 

time: 175 us -> 169 us (0.966)
  Pallas kernels: 171 us -> 164 us
    pallas_call x1, Pallas kernels: 171 us -> 164 us  [local(): pl.pallas_call(functools.partial(step_kernel, dims), out_shape=(jax.Shape...]
where the time goes in v1:
time: 169 us
  Pallas kernels  164 us (97%)
  local copies, waits for them, and re-layouts  3.77 us (2%)
    pallas_call x1, Pallas kernels, local(): pl.pallas_call(functools.partial(step_kernel, dims), out_shape=(jax.Shape...  164 us
    unnamed x4, local copies, waits for them, and re-layouts  3.77 us

profile of v1, /device:TPU:0, one launch (start us, length us, event | category | flops | bytes accessed | tf_op | source)
XLA Modules:
  0.0 168.6 jit_solution(3888079813672890948)
XLA Ops:
  0.6 164.2 %step.1 = (bf16[4,256,1024]{2,1,0:T(8,128)(2,1)}, f32[4,32,256]{2,1,0:T(8,128)}) custom-call(s32[4,169]{1,0:T(4,128)} %refs_0_.1, f32[32,4096]{1,0:T(8,128)} %bitcast.22, f32[4,32,256]{2,1,0:T(8,128)} %bitcast.26, f32[32,1536]{1,0:T(8,128)} %refs_3_.1, f32[256,1536]{1,0:T(8,128)} %refs_4_.1, f32[6,4,1536]{2,1,0:T(4,128)} %bitcast.24, f32[1,4]{1,0:T(1,128)} %refs_6_.1, ...), custom_call_target="tpu_custom_call" | custom-call | tf_op jit(solution)/shard_map/step/pallas_call | solution.py:808
  164.8 0.0 copy-start
  164.8 3.1 %copy.20 = bf16[4,256,1024]{2,1,0:T(8,128)(2,1)} copy(bf16[4,256,1024]{2,1,0:T(8,128)(2,1)} %get-tuple-element.8) | data formatting | bytes 4194304
  167.9 0.0 copy-done
  167.9 0.7 copy.21
Async XLA Ops:
  164.8 3.1 %copy-start = (f32[4,32,256]{2,1,0:T(8,128)S(1)}, f32[4,32,256]{2,1,0:T(8,128)}, u32[]{:S(2)}) copy-start(f32[4,32,256]{2,1,0:T(8,128)} %get-tuple-element.5) | copy-start | bytes 393220

commit v2 on v1

--- a/solution.py
+++ b/solution.py
@@ -388,6 +388,8 @@
         [(matrix, part) for part in range(count)] for matrix, count in enumerate(dims.parts)
     ]
     first = chunks[QKV] + chunks[OUT]
+    up_late = [chunk for chunk in chunks[UP] if chunk not in dims.early]
+    up_early = [chunk for chunk in chunks[UP] if chunk in dims.early]
 
     def begin_y(group):
         for chunk in group:
@@ -490,7 +492,7 @@
         @pl.when(slot == 2)
         def _():
             relay.steps(first, 1)
-            relay.own_z(chunks[UP])
+            relay.own_z(up_late + up_early)
 
         @pl.when(slot == 3)
         def _():
@@ -543,10 +545,7 @@
 
         @pl.when(turn == 2)
         def _():
-            inside(True, lambda: relay.steps(chunks[UP], 1))
-            relay.own_z(chunks[DOWN])
-            relay.cross_z(chunks[DOWN])
-            inside(True, lambda: relay.own_y(chunks[DOWN]))
+            inside(True, lambda: relay.steps(up_late, 1))
 
         def project(tile):
             cols = pl.ds(pl.multiple_of(tile * heads_width, heads_width), heads_width)
@@ -568,18 +567,27 @@
             total = mixed[:, head_size : head_size + 1]
             v.attended[slot, :, low:high] = (mixed[:, :head_size] / total).astype(bf16)
             if head == 1:
-                at_end(turn == 1, lambda: relay.steps(chunks[UP], 0))
-                at_end(turn == 3, lambda: relay.steps(chunks[UP], 1))
-
-        inside(turn == 0, lambda: relay.steps(chunks[UP], 0))
-
-        @pl.when(turn == 1)
-        def _():
-            relay.wait_y_all(chunks[OUT])
-
-        @pl.when(turn > 0)
-        def _():
-            loop(jnp.where(turn == 1, 2, 1), lambda back: project_out(turn - jnp.where(turn == 1, 1, 0) + back))
+                at_end(turn == 1, lambda: relay.steps(up_late, 0))
+
+                @pl.when(turn == 1)
+                def _():
+                    relay.wait_y_all(chunks[OUT])
+                    project_out(turn - 1)
+
+        inside(turn == 0, lambda: relay.steps(up_late + up_early, 0))
+
+        pl.when(turn > 0)(lambda: project_out(turn))
+
+        at_end(turn == 1, lambda: relay.steps(up_early, 0))
+
+        @pl.when(turn == 2)
+        def _():
+            inside(True, lambda: relay.steps(up_early, 1))
+            relay.own_z(chunks[DOWN])
+            relay.cross_z(chunks[DOWN])
+            inside(True, lambda: relay.own_y(chunks[DOWN]))
+            at_end(True, lambda: relay.steps(up_late, 1))
+            at_end(True, lambda: relay.own_y(chunks[DOWN][:3]))
 
     def slot_of(turn):
         return turn // 2 + half * lax.rem(turn, 2)
@@ -626,29 +634,14 @@
 
         @pl.when(j == 0)
         def _():
-            relay.steps(chunks[UP], 2)
-            at_end(True, lambda: relay.own_y(chunks[DOWN]))
+            at_end(True, lambda: relay.steps(up_early, 1))
+            relay.steps(up_late, 2)
+            at_end(True, lambda: relay.own_y(chunks[DOWN][3:]))
             inside(True, lambda: relay.steps(chunks[DOWN], 0))
+            relay.steps(up_early, 2)
 
     loop(half, second_norms, "second_norm")
     relay.wait_y_all(chunks[UP])
-
-    unit_tile = 512
-
-    def lift_units(turn):
-        slot = turn // 2 + half * (1 - lax.rem(turn, 2))
-        pl.when(slot < half)(lambda: swap2(slot).wait_recv())
-
-        def tile_units(tile):
-            cols = pl.ds(pl.multiple_of(tile * unit_tile, unit_tile), unit_tile)
-            lifted = dot(v.normed2[slot], v.w_up[:, cols])
-            v.hidden[slot, :, cols] = jax.nn.gelu(lifted, approximate=True).astype(bf16)
-
-        loop(units // unit_tile, tile_units)
-        at_end(turn == 1, lambda: relay.steps(chunks[DOWN], 0))
-        inside(turn == 1, lambda: relay.steps(chunks[DOWN], 1))
-
-    loop(images, lift_units, "lift_units")
 
     both = jnp.minimum(o, outer - 1 - o)
     sign = jnp.where(o < outer - 1 - o, 1, -1)
@@ -661,18 +654,13 @@
         beyond = o + sign * (n - both)
         return jnp.where(n <= 2 * both, beside, beyond)
 
-    if blocks != outer:
-        at_end(True, lambda: relay.steps(chunks[DOWN], 1))
-        relay.steps(chunks[DOWN], 2)
-        relay.wait_y_all(chunks[DOWN])
-
     def wait_down(n, parts):
         if blocks == outer:
             for chunk in parts:
                 if not relay.crosses_early(chunk):
                     relay.wait_y(chunk, block_of(n))
 
-    def down_piece(n, low, size):
+    def down_piece(n, low, size, first_j=0, count=half):
         start = block_of(n) * block + low
         cols = pl.ds(pl.multiple_of(start, 128), size)
         piece = slice(low, low + size)
@@ -682,7 +670,7 @@
             v.near_out1[n, j, :, piece] = dot_t(v.hidden[j], v.w_down[cols, :]).astype(bf16)
             near1(n, j, piece, turn).start()
 
-        loop(half, theirs)
+        loop(count, lambda j: theirs(first_j + j))
 
         def ours(j):
             partial = dot_t(v.hidden[half + j], v.w_down[cols, :])
@@ -692,7 +680,7 @@
             far1(n, j, piece, turn).start()
             v.stream[j, :, cols] += v.gain[j, :, cols] * pair
 
-        loop(half, ours)
+        loop(count, lambda j: ours(first_j + j))
 
     def add_far(n, j, low, size):
         start = block_of(n) * block + low
@@ -701,9 +689,39 @@
         far1(n, j, piece, low // size).wait_recv()
         v.stream[j, :, cols] += v.gain[j, :, cols] * v.far_in1[n, j, :, piece].astype(f32)
 
+    unit_tile = 512
+
+    def lift_units(turn):
+        slot = turn // 2 + half * (1 - lax.rem(turn, 2))
+        pl.when(slot < half)(lambda: swap2(slot).wait_recv())
+
+        def tile_units(tile):
+            cols = pl.ds(pl.multiple_of(tile * unit_tile, unit_tile), unit_tile)
+            lifted = dot(v.normed2[slot], v.w_up[:, cols])
+            v.hidden[slot, :, cols] = jax.nn.gelu(lifted, approximate=True).astype(bf16)
+
+        loop(units // unit_tile, tile_units)
+        at_end(turn == 1, lambda: relay.steps(chunks[DOWN], 0))
+        inside(turn == 1, lambda: relay.steps(chunks[DOWN], 1))
+        if blocks == outer:
+
+            @pl.when(lax.rem(turn, 2) == 1)
+            def _():
+                pl.when(turn == 1)(lambda: wait_down(0, chunks[DOWN]))
+                down_piece(0, 0, block, turn // 2, 1)
+
+
+    loop(images, lift_units, "lift_units")
+
+    if blocks != outer:
+        at_end(True, lambda: relay.steps(chunks[DOWN], 1))
+        relay.steps(chunks[DOWN], 2)
+        relay.wait_y_all(chunks[DOWN])
+
     most = 2 * len(chunks[DOWN]) // 3
     front, back = chunks[DOWN][:most], chunks[DOWN][most:]
     end = blocks - 1
+    skip = 1 if blocks == outer else 0
     part = block // 3
 
     def down_relays(n, group):
@@ -712,17 +730,18 @@
             pl.when(n == 2)(lambda: relay.steps(group, 2))
 
     def down_block(n):
-        down_relays(n, front)
+        n = n + skip
+        down_relays(n, chunks[DOWN][:3])
         with jax.named_scope("wait_down"):
             wait_down(n, chunks[DOWN])
         down_piece(n, 0, block)
-        down_relays(n, back)
+        down_relays(n, chunks[DOWN][3:])
 
         @pl.when(n > 1)
         def _():
             loop(half, lambda j: add_far(n - 2, j, 0, block))
 
-    loop(end, down_block, "down_block")
+    loop(end - skip, down_block, "down_block")
     with jax.named_scope("last_wait"):
         wait_down(end, front)
     down_piece(end, 0, part)

time: 169 us -> 167 us (0.988)
  Pallas kernels: 164 us -> 162 us
    pallas_call x1, Pallas kernels: 164 us -> 162 us  [local(): pl.pallas_call(functools.partial(step_kernel, dims), out_shape=(jax.Shape...]
where the time goes in v2:
time: 167 us; the launch traced here: 166 us
  Pallas kernels  162 us (97%)
  local copies, waits for them, and re-layouts  3.77 us (2%)
    pallas_call x1, Pallas kernels, local(): pl.pallas_call(functools.partial(step_kernel, dims), out_shape=(jax.Shape...  162 us
    unnamed x4, local copies, waits for them, and re-layouts  3.77 us

profile of v2, /device:TPU:0, one launch (start us, length us, event | category | flops | bytes accessed | tf_op | source)
XLA Modules:
  0.0 166.4 jit_solution(11576677789720592379)
XLA Ops:
  0.6 162.0 %step.1 = (bf16[4,256,1024]{2,1,0:T(8,128)(2,1)}, f32[4,32,256]{2,1,0:T(8,128)}) custom-call(s32[4,169]{1,0:T(4,128)} %refs_0_.1, f32[32,4096]{1,0:T(8,128)} %bitcast.22, f32[4,32,256]{2,1,0:T(8,128)} %bitcast.26, f32[32,1536]{1,0:T(8,128)} %refs_3_.1, f32[256,1536]{1,0:T(8,128)} %refs_4_.1, f32[6,4,1536]{2,1,0:T(4,128)} %bitcast.24, f32[1,4]{1,0:T(1,128)} %refs_6_.1, ...), custom_call_target="tpu_custom_call" | custom-call | tf_op jit(solution)/shard_map/step/pallas_call | solution.py:827
  162.6 0.0 copy-start
  162.6 3.1 %copy.20 = bf16[4,256,1024]{2,1,0:T(8,128)(2,1)} copy(bf16[4,256,1024]{2,1,0:T(8,128)(2,1)} %get-tuple-element.8) | data formatting | bytes 4194304
  165.7 0.0 copy-done
  165.7 0.7 copy.21
Async XLA Ops:
  162.6 3.1 %copy-start = (f32[4,32,256]{2,1,0:T(8,128)S(1)}, f32[4,32,256]{2,1,0:T(8,128)}, u32[]{:S(2)}) copy-start(f32[4,32,256]{2,1,0:T(8,128)} %get-tuple-element.5) | copy-start | bytes 393220

commit v3 on v2

--- a/solution.py
+++ b/solution.py
@@ -487,7 +487,6 @@
         def _():
             relay.cross_z(first)
             relay.steps(first, 0)
-            begin_y(chunks[UP])
 
         @pl.when(slot == 2)
         def _():
@@ -497,6 +496,7 @@
         @pl.when(slot == 3)
         def _():
             relay.steps(first, 2)
+            begin_y(chunks[UP])
             if not relay.crosses_early((OUT, 0)):
                 relay.own_y(chunks[OUT])
                 relay.cross_rest(chunks[OUT])
@@ -510,7 +510,6 @@
     loop(images, embed, "embed")
     canvas_out = pltpu.make_async_copy(v.canvas_v, canvas_hbm, v.store.at[images])
     canvas_out.start()
-    relay.cross_z(chunks[UP])
     relay.wait_y_all(chunks[QKV])
 
     def pair_copy(source, target, lane, recv, t_other):
@@ -567,6 +566,7 @@
             total = mixed[:, head_size : head_size + 1]
             v.attended[slot, :, low:high] = (mixed[:, :head_size] / total).astype(bf16)
             if head == 1:
+                pl.when(turn == 0)(lambda: relay.cross_z(chunks[UP]))
                 at_end(turn == 1, lambda: relay.steps(up_late, 0))
 
                 @pl.when(turn == 1)

time: 167 us -> 168 us (level)
  Pallas kernels: 162 us -> 164 us
    pallas_call x1, Pallas kernels: 162 us -> 164 us  [local(): pl.pallas_call(functools.partial(step_kernel, dims), out_shape=(jax.Shape...]
where the time goes in v3:
time: 168 us
  Pallas kernels  164 us (98%)
  local copies, waits for them, and re-layouts  3.77 us (2%)
    pallas_call x1, Pallas kernels, local(): pl.pallas_call(functools.partial(step_kernel, dims), out_shape=(jax.Shape...  164 us
    unnamed x4, local copies, waits for them, and re-layouts  3.77 us

profile of v3, /device:TPU:0, one launch (start us, length us, event | category | flops | bytes accessed | tf_op | source)
XLA Modules:
  0.0 168.2 jit_solution(7506890450030804691)
XLA Ops:
  0.6 163.7 %step.1 = (bf16[4,256,1024]{2,1,0:T(8,128)(2,1)}, f32[4,32,256]{2,1,0:T(8,128)}) custom-call(s32[4,169]{1,0:T(4,128)} %refs_0_.1, f32[32,4096]{1,0:T(8,128)} %bitcast.22, f32[4,32,256]{2,1,0:T(8,128)} %bitcast.26, f32[32,1536]{1,0:T(8,128)} %refs_3_.1, f32[256,1536]{1,0:T(8,128)} %refs_4_.1, f32[6,4,1536]{2,1,0:T(4,128)} %bitcast.24, f32[1,4]{1,0:T(1,128)} %refs_6_.1, ...), custom_call_target="tpu_custom_call" | custom-call | tf_op jit(solution)/shard_map/step/pallas_call | solution.py:827
  164.4 0.0 copy-start
  164.4 3.1 %copy.20 = bf16[4,256,1024]{2,1,0:T(8,128)(2,1)} copy(bf16[4,256,1024]{2,1,0:T(8,128)(2,1)} %get-tuple-element.8) | data formatting | bytes 4194304
  167.5 0.0 copy-done
  167.5 0.7 copy.21
Async XLA Ops:
  164.4 3.1 %copy-start = (f32[4,32,256]{2,1,0:T(8,128)S(1)}, f32[4,32,256]{2,1,0:T(8,128)}, u32[]{:S(2)}) copy-start(f32[4,32,256]{2,1,0:T(8,128)} %get-tuple-element.5) | copy-start | bytes 393220
